TPU v7x, 32 devices: a whole 2x2x4 slice. The times are simulated.
32 devices in a mesh: lon: 8 (over z, x), ch: 4 (over y, core).
Axes of the slice: x: 2, y: 2, z: 4, core: 2. Of those that a mesh axis runs over, the one named last changes fastest.
Arguments:
- grid_inputs: bfloat16 [230400, 474], P('lon'), may hold values from -6 to 6
- embed_weight: bfloat16 [474, 512], replicated, may hold values from -0.25 to 0.25
- embed_bias: float32 [512], replicated, may hold values from -3 to 3
- mesh_latent: bfloat16 [5120, 512], P('lon', 'ch'), may hold values from -6 to 6
- edge_features: bfloat16 [4, 180224], P(None, 'lon'), may hold values from -6 to 6
- senders: int32 [180224], P('lon'), may hold values from 0 to 230399, as said below
- receivers: int32 [180224], P('lon'), may hold values from 0 to 5119, as said below
- sender_weight: bfloat16 [512, 512], P(None, 'ch'), may hold values from -0.25 to 0.25
- receiver_weight: bfloat16 [512, 512], P(None, 'ch'), may hold values from -0.25 to 0.25
- feature_weight: bfloat16 [4, 512], P(None, 'ch'), may hold values from -3 to 3
- hidden_bias: float32 [512], P('ch'), may hold values from -3 to 3
- message_weight: bfloat16 [512, 512], P('ch'), may hold values from -0.25 to 0.25
- message_bias: float32 [512], replicated, may hold values from -1.2 to 1.2
- norm_gain: float32 [512], P('ch'), may hold values from 0.5 to 1.5
- norm_shift: float32 [512], P('ch'), may hold values from -3 to 3
Outputs:
- mesh_out: bfloat16 [5120, 512], P('lon', 'ch')
Inputs may be any that keep to these rules, and one draw needn't show every extreme that they name: Edge e belongs to block b = e // 22528. Its sender is c * 640 + t with latitude row t and a column c that lies, counted around the closed circle of 360 columns, at most 4 columns before or after the block's own columns b * 45 to b * 45 + 44; some block reaches 4 columns on both sides. Within each aligned run of min(2048, 22528) edges of a block, the senders' columns, counted from the block's first widened column, lie within 7 consecutive columns. `receivers`: the receiver of edge e lies among the mesh nodes b * 640 to b * 640 + 639 of its block b = e // 22528; a mesh node may receive no edge.
All inputs are finite; a program needn't handle non-finite values.
Results may differ from a plain program's by a relative error of at most 0.0028.
Values may be sent and summed in bfloat16 or wider, within the bound.
A program may use at most 128 MiB of HBM per device.

v0:
```python
import jax
import jax.numpy as jnp
from jax import lax
from jax.sharding import PartitionSpec as P

LAT = 640
HALO = 4


def with_halo(block, sides, width):
    for axis, dim in sides:
        count = lax.axis_size(axis)
        forward = [(i, i + 1) for i in range(count - 1)]
        forward.append((count - 1, 0))
        backward = [(target, source) for source, target in forward]
        low = lax.ppermute(
            lax.slice_in_dim(block, block.shape[dim] - width, None, axis=dim), axis, forward
        )
        high = lax.ppermute(lax.slice_in_dim(block, 0, width, axis=dim), axis, backward)
        block = jnp.concatenate([low, block, high], axis=dim)
    return block


def embedded(grid_rows, embed_weight, embed_bias):
    return jax.nn.silu(
        jnp.dot(grid_rows, embed_weight, preferred_element_type=jnp.float32) + embed_bias
    ).astype(jnp.bfloat16)


def on_device(
    grid_inputs,
    embed_weight,
    embed_bias,
    mesh_latent,
    edge_features,
    senders,
    receivers,
    sender_weight,
    receiver_weight,
    feature_weight,
    hidden_bias,
    message_weight,
    message_bias,
    norm_gain,
    norm_shift,
):
    lon_count = lax.axis_size("lon")
    lon_place = lax.axis_index("lon")
    ch_place = lax.axis_index("ch")
    columns = grid_inputs.shape[0] // LAT
    mesh_nodes = mesh_latent.shape[0]
    share_width = mesh_latent.shape[1]
    full_width = message_weight.shape[1]
    latent = embedded(grid_inputs, embed_weight, embed_bias)
    own_terms = jnp.dot(latent, sender_weight, preferred_element_type=jnp.float32)
    widened = with_halo(own_terms.reshape(columns, LAT, share_width), (("lon", 0),), HALO)
    sent_terms = widened.reshape(-1, share_width)
    grid_column = senders // LAT
    shifted = jnp.mod(grid_column - lon_place * columns + HALO, columns * lon_count)
    local_send = shifted * LAT + senders % LAT
    local_recv = receivers - lon_place * mesh_nodes
    full_mesh = lax.all_gather(mesh_latent, "ch", axis=1, tiled=True)
    recv_terms = jnp.dot(full_mesh, receiver_weight, preferred_element_type=jnp.float32)
    edge_count = senders.shape[0]
    block_rows = min(2048, edge_count)
    steps_count = edge_count // block_rows
    feature_blocks = jnp.transpose(
        edge_features.reshape(edge_features.shape[0], steps_count, block_rows), (1, 0, 2)
    )
    node_ids = lax.broadcasted_iota(jnp.int32, (1, mesh_nodes), 1)

    def accumulate(carried, pieces):
        totals, tallies = carried
        send_ids, recv_ids, features = pieces
        before = jnp.take(sent_terms, send_ids, axis=0) + jnp.take(recv_terms, recv_ids, axis=0)
        before = (
            before
            + lax.dot_general(
                features,
                feature_weight,
                (((0,), (0,)), ((), ())),
                preferred_element_type=jnp.float32,
            )
            + hidden_bias
        )
        hidden = jax.nn.silu(before).astype(jnp.bfloat16)
        one_hot = (recv_ids[:, None] == node_ids).astype(jnp.bfloat16)
        totals = totals + lax.dot_general(
            one_hot, hidden, (((0,), (0,)), ((), ())), preferred_element_type=jnp.float32
        )
        tallies = tallies + jnp.sum(one_hot, axis=0, dtype=jnp.float32)
        return ((totals, tallies), None)

    start = (
        jnp.zeros((mesh_nodes, share_width), jnp.float32),
        jnp.zeros((mesh_nodes,), jnp.float32),
    )
    pieces_all = (
        local_send.reshape(steps_count, block_rows),
        local_recv.reshape(steps_count, block_rows),
        feature_blocks,
    )
    (totals, tallies), ignored = lax.scan(accumulate, start, pieces_all)
    partial_value = jnp.dot(
        totals, message_weight.astype(jnp.float32), precision=lax.Precision.HIGHEST
    )
    bias_share = lax.dynamic_slice_in_dim(message_bias, ch_place * share_width, share_width, 0)
    node_share = (
        lax.psum_scatter(partial_value, "ch", scatter_dimension=1, tiled=True)
        + tallies[:, None] * bias_share
    )
    centre = lax.psum(jnp.sum(node_share, axis=1, keepdims=True), "ch") / full_width
    spread = (
        lax.psum(jnp.sum(jnp.square(node_share - centre), axis=1, keepdims=True), "ch") / full_width
    )
    normed = (node_share - centre) * lax.rsqrt(spread + 1.0)
    return (mesh_latent.astype(jnp.float32) + normed * norm_gain + norm_shift).astype(jnp.bfloat16)


def solution(mesh):
    return jax.shard_map(
        on_device,
        mesh=mesh,
        in_specs=(
            P("lon", None),
            P(),
            P(),
            P("lon", "ch"),
            P(None, "lon"),
            P("lon"),
            P("lon"),
            P(None, "ch"),
            P(None, "ch"),
            P(None, "ch"),
            P("ch"),
            P("ch", None),
            P(),
            P("ch"),
            P("ch"),
        ),
        out_specs=P("lon", "ch"),
        check_vma=False,
    )
```

profile of v0, /device:TPU:0, one launch (start us, length us, event | category | flops | bytes accessed | tf_op | source)
XLA Modules:
  0.0 416.3 jit_solution(979009303681830527)
XLA Ops:
  6.5 1.0 copy-done
  7.6 31.8 %multiply_convert_fusion.1 = bf16[28800,512]{1,0:T(8,128)(2,1)} fusion(bf16[28800,474]{0,1:T(8,128)(2,1)} %param.17, bf16[474,512]{1,0:T(8,128)(2,1)S(1)} %copy-done, f32[512]{0:T(512)} %param.19), kind=kOutput, calls=%fused_computation.33 | convolution fusion | flops 14067302400 | bytes 57281024 | tf_op jit(solution)/shard_map/dot_general | solution.py:26
  39.4 16.5 %fusion.28 = f32[28800,128]{1,0:T(8,128)} fusion(bf16[28800,512]{1,0:T(8,128)(2,1)} %multiply_convert_fusion.1, bf16[512,128]{1,0:T(8,128)(2,1)S(1)} %copy-done.5), kind=kOutput, calls=%fused_computation.53 | convolution fusion | flops 3774873600 | bytes 44367872 | tf_op jit(solution)/shard_map/dot_general | solution.py:55
  55.8 3.4 fusion.27
  59.2 3.0 collective-permute-start
  62.2 3.0 collective-permute-start.1
  65.5 8.1 %all_gather.3 = bf16[640,512]{1,0:T(8,128)(2,1)S(1)} all-gather(bf16[640,128]{1,0:T(8,128)(2,1)S(1)} %copy-done.2), channel_id=1, replica_groups=mesh['lon'=8,'ch'=4] {'ch'}, dimensions={1}, use_global_device_ids=true | all-gather | bytes 819200 | tf_op jit(solution)/shard_map/all_gather | solution.py:62
  73.6 0.3 fusion.29
  74.0 44.7 %collective-permute-done = f32[4,640,128]{2,1,0:T(8,128)S(1)} collective-permute-done((f32[4,640,128]{2,1,0:T(8,128)}, f32[4,640,128]{2,1,0:T(8,128)S(1)}, u32[]{:S(2)}, u32[]{:S(2)}) %collective-permute-start) | collective-permute-done | bytes 1310752 | tf_op jit(solution)/shard_map/ppermute | solution.py:16
  118.6 2.1 collective-permute-done.1
  120.7 10.9 %pad_maximum_fusion = f32[53,640,128]{2,1,0:T(8,128)} fusion(f32[4,640,128]{2,1,0:T(8,128)S(1)} %collective-permute-done.1, f32[45,640,128]{2,1,0:T(8,128)} %bitcast.43, f32[4,640,128]{2,1,0:T(8,128)S(1)} %collective-permute-done), kind=kLoop, calls=%fused_computation.34 | loop fusion | flops 8683520 | bytes 34734080 | tf_op jit(solution)/shard_map/concatenate | solution.py:20
  131.7 232.3 %while.13 = (s32[]{:T(128)}, f32[640,128]{1,0:T(8,128)}, f32[640]{0:T(1024)S(1)}, s32[11,2048]{1,0:T(8,128)S(1)}, s32[11,2048]{1,0:T(8,128)S(1)}, /*index=5*/f32...) while((s32[]{:T(128)}, f32[640,128]{1,0:T(8,128)}, ...), condition=%wide.region_2.3_spmd.clone, body=%wide.region_0.2_spmd.clone.sunk | while | flops 347021952 | bytes 9736380 | solution.py:103
  131.8 5.5 %gather_fusion = f32[2048,128]{1,0:T(8,128)S(1)} fusion(f32[640,128]{1,0:T(8,128)S(1)} %get-tuple-element.227, s32[2048]{0:T(1024)S(1)} %broadcast_clamp_fusion.4), kind=kCustom, calls=%fused_computation.1.clone.clone.1 | custom fusion | bytes 2105344 | tf_op jit(solution)/shard_map/while/body/eval_jaxpr/jit(_take)/gather | solution.py:75
  137.3 11.4 %gather_fusion.1 = f32[2048,128]{1,0:T(8,128)S(1)} fusion(f32[33920,128]{1,0:T(8,128)} %get-tuple-element.226, s32[2048]{0:T(1024)S(1)} %broadcast_clamp_fusion.5), kind=kCustom, calls=%fused_computation.clone.clone.1 | custom fusion | bytes 2105344 | tf_op jit(solution)/shard_map/while/body/eval_jaxpr/jit(_take)/gather | solution.py:75
  148.7 3.4 fusion.45
  152.1 0.7 convert_reduce_fusion.2
  152.9 5.5 %gather_fusion = f32[2048,128]{1,0:T(8,128)S(1)} fusion(f32[640,128]{1,0:T(8,128)S(1)} %get-tuple-element.227, s32[2048]{0:T(1024)S(1)} %broadcast_clamp_fusion.4), kind=kCustom, calls=%fused_computation.1.clone.clone.1 | custom fusion | bytes 2105344 | tf_op jit(solution)/shard_map/while/body/eval_jaxpr/jit(_take)/gather | solution.py:75
  158.4 11.4 %gather_fusion.1 = f32[2048,128]{1,0:T(8,128)S(1)} fusion(f32[33920,128]{1,0:T(8,128)} %get-tuple-element.226, s32[2048]{0:T(1024)S(1)} %broadcast_clamp_fusion.5), kind=kCustom, calls=%fused_computation.clone.clone.1 | custom fusion | bytes 2105344 | tf_op jit(solution)/shard_map/while/body/eval_jaxpr/jit(_take)/gather | solution.py:75
  169.8 3.4 fusion.45
  173.2 0.7 convert_reduce_fusion.2
  174.0 5.5 %gather_fusion = f32[2048,128]{1,0:T(8,128)S(1)} fusion(f32[640,128]{1,0:T(8,128)S(1)} %get-tuple-element.227, s32[2048]{0:T(1024)S(1)} %broadcast_clamp_fusion.4), kind=kCustom, calls=%fused_computation.1.clone.clone.1 | custom fusion | bytes 2105344 | tf_op jit(solution)/shard_map/while/body/eval_jaxpr/jit(_take)/gather | solution.py:75
  179.5 11.4 %gather_fusion.1 = f32[2048,128]{1,0:T(8,128)S(1)} fusion(f32[33920,128]{1,0:T(8,128)} %get-tuple-element.226, s32[2048]{0:T(1024)S(1)} %broadcast_clamp_fusion.5), kind=kCustom, calls=%fused_computation.clone.clone.1 | custom fusion | bytes 2105344 | tf_op jit(solution)/shard_map/while/body/eval_jaxpr/jit(_take)/gather | solution.py:75
  191.0 3.4 fusion.45
  194.3 0.7 convert_reduce_fusion.2
  195.1 5.5 %gather_fusion = f32[2048,128]{1,0:T(8,128)S(1)} fusion(f32[640,128]{1,0:T(8,128)S(1)} %get-tuple-element.227, s32[2048]{0:T(1024)S(1)} %broadcast_clamp_fusion.4), kind=kCustom, calls=%fused_computation.1.clone.clone.1 | custom fusion | bytes 2105344 | tf_op jit(solution)/shard_map/while/body/eval_jaxpr/jit(_take)/gather | solution.py:75
  200.6 11.4 %gather_fusion.1 = f32[2048,128]{1,0:T(8,128)S(1)} fusion(f32[33920,128]{1,0:T(8,128)} %get-tuple-element.226, s32[2048]{0:T(1024)S(1)} %broadcast_clamp_fusion.5), kind=kCustom, calls=%fused_computation.clone.clone.1 | custom fusion | bytes 2105344 | tf_op jit(solution)/shard_map/while/body/eval_jaxpr/jit(_take)/gather | solution.py:75
  212.1 3.4 fusion.45
  215.5 0.7 convert_reduce_fusion.2
  216.3 5.5 %gather_fusion = f32[2048,128]{1,0:T(8,128)S(1)} fusion(f32[640,128]{1,0:T(8,128)S(1)} %get-tuple-element.227, s32[2048]{0:T(1024)S(1)} %broadcast_clamp_fusion.4), kind=kCustom, calls=%fused_computation.1.clone.clone.1 | custom fusion | bytes 2105344 | tf_op jit(solution)/shard_map/while/body/eval_jaxpr/jit(_take)/gather | solution.py:75
  221.8 11.4 %gather_fusion.1 = f32[2048,128]{1,0:T(8,128)S(1)} fusion(f32[33920,128]{1,0:T(8,128)} %get-tuple-element.226, s32[2048]{0:T(1024)S(1)} %broadcast_clamp_fusion.5), kind=kCustom, calls=%fused_computation.clone.clone.1 | custom fusion | bytes 2105344 | tf_op jit(solution)/shard_map/while/body/eval_jaxpr/jit(_take)/gather | solution.py:75
  233.2 3.4 fusion.45
  236.6 0.7 convert_reduce_fusion.2
  237.4 5.5 %gather_fusion = f32[2048,128]{1,0:T(8,128)S(1)} fusion(f32[640,128]{1,0:T(8,128)S(1)} %get-tuple-element.227, s32[2048]{0:T(1024)S(1)} %broadcast_clamp_fusion.4), kind=kCustom, calls=%fused_computation.1.clone.clone.1 | custom fusion | bytes 2105344 | tf_op jit(solution)/shard_map/while/body/eval_jaxpr/jit(_take)/gather | solution.py:75
  242.9 11.4 %gather_fusion.1 = f32[2048,128]{1,0:T(8,128)S(1)} fusion(f32[33920,128]{1,0:T(8,128)} %get-tuple-element.226, s32[2048]{0:T(1024)S(1)} %broadcast_clamp_fusion.5), kind=kCustom, calls=%fused_computation.clone.clone.1 | custom fusion | bytes 2105344 | tf_op jit(solution)/shard_map/while/body/eval_jaxpr/jit(_take)/gather | solution.py:75
  254.3 3.4 fusion.45
  257.7 0.7 convert_reduce_fusion.2
  258.5 5.5 %gather_fusion = f32[2048,128]{1,0:T(8,128)S(1)} fusion(f32[640,128]{1,0:T(8,128)S(1)} %get-tuple-element.227, s32[2048]{0:T(1024)S(1)} %broadcast_clamp_fusion.4), kind=kCustom, calls=%fused_computation.1.clone.clone.1 | custom fusion | bytes 2105344 | tf_op jit(solution)/shard_map/while/body/eval_jaxpr/jit(_take)/gather | solution.py:75
  264.0 11.4 %gather_fusion.1 = f32[2048,128]{1,0:T(8,128)S(1)} fusion(f32[33920,128]{1,0:T(8,128)} %get-tuple-element.226, s32[2048]{0:T(1024)S(1)} %broadcast_clamp_fusion.5), kind=kCustom, calls=%fused_computation.clone.clone.1 | custom fusion | bytes 2105344 | tf_op jit(solution)/shard_map/while/body/eval_jaxpr/jit(_take)/gather | solution.py:75
  275.4 3.4 fusion.45
  278.8 0.7 convert_reduce_fusion.2
  279.6 5.5 %gather_fusion = f32[2048,128]{1,0:T(8,128)S(1)} fusion(f32[640,128]{1,0:T(8,128)S(1)} %get-tuple-element.227, s32[2048]{0:T(1024)S(1)} %broadcast_clamp_fusion.4), kind=kCustom, calls=%fused_computation.1.clone.clone.1 | custom fusion | bytes 2105344 | tf_op jit(solution)/shard_map/while/body/eval_jaxpr/jit(_take)/gather | solution.py:75
  285.1 11.4 %gather_fusion.1 = f32[2048,128]{1,0:T(8,128)S(1)} fusion(f32[33920,128]{1,0:T(8,128)} %get-tuple-element.226, s32[2048]{0:T(1024)S(1)} %broadcast_clamp_fusion.5), kind=kCustom, calls=%fused_computation.clone.clone.1 | custom fusion | bytes 2105344 | tf_op jit(solution)/shard_map/while/body/eval_jaxpr/jit(_take)/gather | solution.py:75
  296.5 3.4 fusion.45
  299.9 0.7 convert_reduce_fusion.2
  300.7 5.5 %gather_fusion = f32[2048,128]{1,0:T(8,128)S(1)} fusion(f32[640,128]{1,0:T(8,128)S(1)} %get-tuple-element.227, s32[2048]{0:T(1024)S(1)} %broadcast_clamp_fusion.4), kind=kCustom, calls=%fused_computation.1.clone.clone.1 | custom fusion | bytes 2105344 | tf_op jit(solution)/shard_map/while/body/eval_jaxpr/jit(_take)/gather | solution.py:75
  306.2 11.4 %gather_fusion.1 = f32[2048,128]{1,0:T(8,128)S(1)} fusion(f32[33920,128]{1,0:T(8,128)} %get-tuple-element.226, s32[2048]{0:T(1024)S(1)} %broadcast_clamp_fusion.5), kind=kCustom, calls=%fused_computation.clone.clone.1 | custom fusion | bytes 2105344 | tf_op jit(solution)/shard_map/while/body/eval_jaxpr/jit(_take)/gather | solution.py:75
  317.7 3.4 fusion.45
  321.0 0.7 convert_reduce_fusion.2
  321.9 5.5 %gather_fusion = f32[2048,128]{1,0:T(8,128)S(1)} fusion(f32[640,128]{1,0:T(8,128)S(1)} %get-tuple-element.227, s32[2048]{0:T(1024)S(1)} %broadcast_clamp_fusion.4), kind=kCustom, calls=%fused_computation.1.clone.clone.1 | custom fusion | bytes 2105344 | tf_op jit(solution)/shard_map/while/body/eval_jaxpr/jit(_take)/gather | solution.py:75
  327.3 11.4 %gather_fusion.1 = f32[2048,128]{1,0:T(8,128)S(1)} fusion(f32[33920,128]{1,0:T(8,128)} %get-tuple-element.226, s32[2048]{0:T(1024)S(1)} %broadcast_clamp_fusion.5), kind=kCustom, calls=%fused_computation.clone.clone.1 | custom fusion | bytes 2105344 | tf_op jit(solution)/shard_map/while/body/eval_jaxpr/jit(_take)/gather | solution.py:75
  338.8 3.4 fusion.45
  342.2 0.7 convert_reduce_fusion.2
  343.0 5.5 %gather_fusion = f32[2048,128]{1,0:T(8,128)S(1)} fusion(f32[640,128]{1,0:T(8,128)S(1)} %get-tuple-element.227, s32[2048]{0:T(1024)S(1)} %broadcast_clamp_fusion.4), kind=kCustom, calls=%fused_computation.1.clone.clone.1 | custom fusion | bytes 2105344 | tf_op jit(solution)/shard_map/while/body/eval_jaxpr/jit(_take)/gather | solution.py:75
  348.5 11.4 %gather_fusion.1 = f32[2048,128]{1,0:T(8,128)S(1)} fusion(f32[33920,128]{1,0:T(8,128)} %get-tuple-element.226, s32[2048]{0:T(1024)S(1)} %broadcast_clamp_fusion.5), kind=kCustom, calls=%fused_computation.clone.clone.1 | custom fusion | bytes 2105344 | tf_op jit(solution)/shard_map/while/body/eval_jaxpr/jit(_take)/gather | solution.py:75
  359.9 3.4 fusion.45
  363.3 0.7 convert_reduce_fusion.2
  364.0 2.8 fusion.30
  366.8 0.8 dynamic_slice.14
  367.6 25.8 %reduce-scatter.2.cloned.1.call-done = f32[640,128]{1,0:T(8,128)} async-done(((f32[640,512]{1,0:T(8,128)}), f32[640,128]{1,0:T(8,128)}) %reduce-scatter.2.cloned.1.call-update) | async-done | bytes 327696 | tf_op jit(solution)/shard_map/reduce_scatter | solution.py:109
  393.4 1.2 fusion.20
  394.6 5.8 %psum.14 = f32[640,1]{0,1:T(1,128)S(1)} all-reduce(f32[640,1]{0,1:T(1,128)S(1)} %broadcast_in_dim.39), channel_id=1, replica_groups=mesh['lon'=8,'ch'=4] {'ch'}, use_global_device_ids=true, to_apply=%region_5.6 | all-reduce | flops 640 | bytes 5120 | tf_op jit(solution)/shard_map/psum | solution.py:112
  400.4 1.3 multiply_reduce_fusion
  401.8 5.7 %psum.15 = f32[640,1]{0,1:T(1,128)S(1)} all-reduce(f32[640,1]{0,1:T(1,128)S(1)} %broadcast_in_dim.40), channel_id=1, replica_groups=mesh['lon'=8,'ch'=4] {'ch'}, use_global_device_ids=true, to_apply=%region_7.8 | all-reduce | flops 640 | bytes 5120 | tf_op jit(solution)/shard_map/psum | solution.py:114
  407.5 2.0 add_convert_fusion
  (145 shorter events, 1.3 us)
Async XLA Ops:
  6.5 1.0 copy-start
  6.5 32.8 %copy-start.5 = (bf16[512,128]{1,0:T(8,128)(2,1)S(1)}, bf16[512,128]{1,0:T(8,128)(2,1)}, u32[]{:S(2)}) copy-start(bf16[512,128]{1,0:T(8,128)(2,1)} %param.24) | copy-start | bytes 393220
  6.5 386.8 %reduce-scatter.2.cloned.1.call-start = ((), (), s32[]{:S(2)}) async-start(), calls=%async_computation.1 | async-start | bytes 1638400 | tf_op jit(solution)/shard_map/reduce_scatter | solution.py:109
  39.3 25.9 %copy-start.8 = (s32[22528]{0:T(1024)S(1)}, s32[22528]{0:T(1024)}, u32[]{:S(2)}) copy-start(s32[22528]{0:T(1024)} %param.23) | copy-start | bytes 270340
  39.3 26.0 %copy-start.9 = (s32[22528]{0:T(1024)S(1)}, s32[22528]{0:T(1024)}, u32[]{:S(2)}) copy-start(s32[22528]{0:T(1024)} %param.22) | copy-start | bytes 270340
  39.3 26.2 %copy-start.2 = (bf16[640,128]{1,0:T(8,128)(2,1)S(1)}, bf16[640,128]{1,0:T(8,128)(2,1)}, u32[]{:S(2)}) copy-start(bf16[640,128]{1,0:T(8,128)(2,1)} %param.20) | copy-start | bytes 491524
  39.3 34.3 %copy-start.6 = (bf16[512,128]{1,0:T(8,128)(2,1)S(1)}, bf16[512,128]{1,0:T(8,128)(2,1)}, u32[]{:S(2)}) copy-start(bf16[512,128]{1,0:T(8,128)(2,1)} %param.25) | copy-start | bytes 393220
  59.2 59.4 %collective-permute-start = (f32[4,640,128]{2,1,0:T(8,128)}, f32[4,640,128]{2,1,0:T(8,128)S(1)}, u32[]{:S(2)}, u32[]{:S(2)}) collective-permute-start(f32[4,640,128]{2,1,0:T(8,128)} %bitcast), channel_id=1, source_target_pairs={{0,4},{4,8},{8,12},{12,16},{16,20},{20,24},{24,28},{28,0},{1,5},{5... | collective-permute-start | bytes 3932168 | tf_op jit(solution)/shard_map/ppermute | solution.py:16
  62.2 58.5 %collective-permute-start.1 = (f32[4,640,128]{2,1,0:T(8,128)}, f32[4,640,128]{2,1,0:T(8,128)S(1)}, u32[]{:S(2)}, u32[]{:S(2)}) collective-permute-start(f32[4,640,128]{2,1,0:T(8,128)} %bitcast.2), channel_id=1, source_target_pairs={{4,0},{8,4},{12,8},{16,12},{20,16},{24,20},{28,24},{0,28},{5,1},{9... | collective-permute-start | bytes 3932168 | tf_op jit(solution)/shard_map/ppermute | solution.py:19
  120.7 10.9 %copy-start.12 = (bf16[4,128]{1,0:T(4,128)(2,1)S(1)}, bf16[4,128]{1,0:T(4,128)(2,1)}, u32[]{:S(2)}) copy-start(bf16[4,128]{1,0:T(4,128)(2,1)} %param.26) | copy-start | bytes 3076
  120.7 10.9 %copy-start.13 = (f32[128]{0:T(128)S(1)}, f32[128]{0:T(128)}, u32[]{:S(2)}) copy-start(f32[128]{0:T(128)} %param.27) | copy-start | bytes 1540
  131.7 232.3 %copy-start.7 = (bf16[128,512]{1,0:T(8,128)(2,1)S(1)}, bf16[128,512]{1,0:T(8,128)(2,1)}, u32[]{:S(2)}) copy-start(bf16[128,512]{1,0:T(8,128)(2,1)} %param.28) | copy-start | bytes 393220
  131.7 275.8 %copy-start.10 = (f32[128]{0:T(128)S(1)}, f32[128]{0:T(128)}, u32[]{:S(2)}) copy-start(f32[128]{0:T(128)} %param.31) | copy-start | bytes 1540
  131.7 275.8 %copy-start.11 = (f32[128]{0:T(128)S(1)}, f32[128]{0:T(128)}, u32[]{:S(2)}) copy-start(f32[128]{0:T(128)} %param.30) | copy-start | bytes 1540
  131.7 17.0 %copy-start.3 = (f32[640,128]{1,0:T(8,128)S(1)}, f32[640,128]{1,0:T(8,128)}, u32[]{:S(2)}) copy-start(f32[640,128]{1,0:T(8,128)} %get-tuple-element.210) | copy-start | bytes 983044 | tf_op jit(solution)/shard_map/while
  152.1 0.7 copy-start.4
  152.8 17.0 %copy-start.3 = (f32[640,128]{1,0:T(8,128)S(1)}, f32[640,128]{1,0:T(8,128)}, u32[]{:S(2)}) copy-start(f32[640,128]{1,0:T(8,128)} %get-tuple-element.210) | copy-start | bytes 983044 | tf_op jit(solution)/shard_map/while
  173.2 0.7 copy-start.4
  173.9 17.0 %copy-start.3 = (f32[640,128]{1,0:T(8,128)S(1)}, f32[640,128]{1,0:T(8,128)}, u32[]{:S(2)}) copy-start(f32[640,128]{1,0:T(8,128)} %get-tuple-element.210) | copy-start | bytes 983044 | tf_op jit(solution)/shard_map/while
  194.3 0.7 copy-start.4
  195.1 17.0 %copy-start.3 = (f32[640,128]{1,0:T(8,128)S(1)}, f32[640,128]{1,0:T(8,128)}, u32[]{:S(2)}) copy-start(f32[640,128]{1,0:T(8,128)} %get-tuple-element.210) | copy-start | bytes 983044 | tf_op jit(solution)/shard_map/while
  215.5 0.7 copy-start.4
  216.2 17.0 %copy-start.3 = (f32[640,128]{1,0:T(8,128)S(1)}, f32[640,128]{1,0:T(8,128)}, u32[]{:S(2)}) copy-start(f32[640,128]{1,0:T(8,128)} %get-tuple-element.210) | copy-start | bytes 983044 | tf_op jit(solution)/shard_map/while
  236.6 0.7 copy-start.4
  237.3 17.0 %copy-start.3 = (f32[640,128]{1,0:T(8,128)S(1)}, f32[640,128]{1,0:T(8,128)}, u32[]{:S(2)}) copy-start(f32[640,128]{1,0:T(8,128)} %get-tuple-element.210) | copy-start | bytes 983044 | tf_op jit(solution)/shard_map/while
  257.7 0.7 copy-start.4
  258.4 17.0 %copy-start.3 = (f32[640,128]{1,0:T(8,128)S(1)}, f32[640,128]{1,0:T(8,128)}, u32[]{:S(2)}) copy-start(f32[640,128]{1,0:T(8,128)} %get-tuple-element.210) | copy-start | bytes 983044 | tf_op jit(solution)/shard_map/while
  278.8 0.7 copy-start.4
  279.5 17.0 %copy-start.3 = (f32[640,128]{1,0:T(8,128)S(1)}, f32[640,128]{1,0:T(8,128)}, u32[]{:S(2)}) copy-start(f32[640,128]{1,0:T(8,128)} %get-tuple-element.210) | copy-start | bytes 983044 | tf_op jit(solution)/shard_map/while
  299.9 0.7 copy-start.4
  300.7 17.0 %copy-start.3 = (f32[640,128]{1,0:T(8,128)S(1)}, f32[640,128]{1,0:T(8,128)}, u32[]{:S(2)}) copy-start(f32[640,128]{1,0:T(8,128)} %get-tuple-element.210) | copy-start | bytes 983044 | tf_op jit(solution)/shard_map/while
  321.0 0.7 copy-start.4
  321.8 17.0 %copy-start.3 = (f32[640,128]{1,0:T(8,128)S(1)}, f32[640,128]{1,0:T(8,128)}, u32[]{:S(2)}) copy-start(f32[640,128]{1,0:T(8,128)} %get-tuple-element.210) | copy-start | bytes 983044 | tf_op jit(solution)/shard_map/while
  342.2 0.7 copy-start.4
  342.9 17.0 %copy-start.3 = (f32[640,128]{1,0:T(8,128)S(1)}, f32[640,128]{1,0:T(8,128)}, u32[]{:S(2)}) copy-start(f32[640,128]{1,0:T(8,128)} %get-tuple-element.210) | copy-start | bytes 983044 | tf_op jit(solution)/shard_map/while
  363.3 0.7 copy-start.4
  364.0 45.4 %copy-start.1 = (bf16[474,512]{1,0:T(8,128)(2,1)S(1)}, bf16[474,512]{1,0:T(8,128)(2,1)}, u32[]{:S(2)}) copy-start(bf16[474,512]{1,0:T(8,128)(2,1)} %param.18) | copy-start | bytes 1456132
Sparse Core Ops, SparseCore 0:
  366.9 26.4 reduce-scatter.1
where the time goes:
time: 418 us; the launch traced here: 416 us
  local copies, waits for them, and re-layouts  191 us (46%)
  matrix products  88.5 us (21%)
  waiting for transfers between devices  72.6 us (17%)
  other arithmetic  23.9 us (6%)
  blocking collectives  19.6 us (5%)
  between operations  13.6 us (3%)
  starting transfers between devices  6 us (1%)
    gather x11, local copies, waits for them, and re-layouts, accumulate(): jnp.take(sent_terms, send_ids, axis=0)  125 us
    gather x11, local copies, waits for them, and re-layouts, accumulate(): jnp.take(recv_terms, recv_ids, axis=0)  60.1 us
    ppermute x1, waiting for transfers between devices, with_halo(): lax.ppermute(lax.slice_in_dim(block, block.shape[dim] - width, None, axis...  44.7 us
    dot_general x11, matrix products, accumulate(): lax.dot_general(one_hot, hidden, (((0,), (0,)), ((), ())), preferred_elem...  37.1 us
    dot_general x1, matrix products, embedded(): jnp.dot(grid_rows, embed_weight, preferred_element_type=jnp.float32)  31.8 us
    reduce_scatter x1, waiting for transfers between devices, on_device(): lax.psum_scatter(partial_value, 'ch', scatter_dimension=1, tiled=True)  25.8 us
    dot_general x1, matrix products, on_device(): jnp.dot(latent, sender_weight, preferred_element_type=jnp.float32)  16.5 us
    concatenate x1, other arithmetic, with_halo(): block = jnp.concatenate([low, block, high], axis=dim)  10.9 us
  transfers between devices with their start and end apart: 3, of which 3 were waited for; matrix products, arithmetic and copies ran while one was open for 0% of the time, Pallas kernels for 0%

commit v1 on v0

v1 whole, which is shorter than its diff:
```python
import functools

import jax
import jax.numpy as jnp
from jax import lax
from jax.experimental import pallas as pl
from jax.experimental.pallas import tpu as pltpu
from jax.sharding import PartitionSpec as P

LAT = 640
HALO = 4
CHUNK = 256


def silu(v):
    half = 0.5 * v
    return half + half * jnp.tanh(half)


def dense_kernel(x_ref, embed_ref, bias_ref, sender_ref, out_ref):
    before = (
        jnp.dot(x_ref[...], embed_ref[...], preferred_element_type=jnp.float32) + bias_ref[...]
    )
    latent = silu(before).astype(jnp.bfloat16)
    out_ref[...] = jnp.dot(
        latent, sender_ref[...], preferred_element_type=jnp.float32
    ).astype(out_ref.dtype)


def sender_terms(grid_inputs, embed_weight, embed_bias, sender_weight, rows, steps, place, dtype):
    channels, full_width = embed_weight.shape
    width = sender_weight.shape[1]
    whole = lambda shape: pl.BlockSpec(shape, lambda i: (0, 0))
    return pl.pallas_call(
        dense_kernel,
        grid=(steps,),
        in_specs=[
            pl.BlockSpec((rows, channels), lambda i: (place(i), 0)),
            whole((channels, full_width)),
            whole((1, full_width)),
            whole((full_width, width)),
        ],
        out_specs=pl.BlockSpec((rows, width), lambda i: (i, 0)),
        out_shape=jax.ShapeDtypeStruct((steps * rows, width), dtype),
        compiler_params=pltpu.CompilerParams(vmem_limit_bytes=48 << 20),
        cost_estimate=pl.CostEstimate(
            flops=2 * steps * rows * full_width * (channels + width),
            bytes_accessed=steps * rows * (2 * channels + 4 * width),
            transcendentals=steps * rows * full_width,
        ),
    )(grid_inputs, embed_weight, embed_bias.reshape(1, -1), sender_weight)


def edge_kernel(
    send_ref,
    recv_ref,
    own_ref,
    low_ref,
    high_ref,
    recv_terms_ref,
    recv_row_ref,
    features_ref,
    feature_weight_ref,
    out_ref,
    table,
    even,
    odd,
    total,
    sems,
):
    own_rows = own_ref.shape[0]
    halo_rows = low_ref.shape[0]
    pieces = ((low_ref, 0), (own_ref, halo_rows), (high_ref, halo_rows + own_rows))
    copies = [
        pltpu.make_async_copy(ref, table.at[pl.ds(at, ref.shape[0])], sems.at[n])
        for n, (ref, at) in enumerate(pieces)
    ]
    for copy in copies:
        copy.start()
    nodes = recv_terms_ref.shape[0]
    total[...] = jnp.zeros_like(total)
    for copy in copies:
        copy.wait()
    chunks = recv_row_ref.shape[1] // CHUNK
    width = recv_terms_ref.shape[1]

    def gather(chunk, held):
        base = chunk * CHUNK
        for i in range(CHUNK):
            held[pl.ds(i, 1), :] = (
                table[pl.ds(send_ref[base + i], 1), :]
                + recv_terms_ref[pl.ds(recv_ref[base + i], 1), :]
            )

    def add_up(chunk, held):
        lanes = pl.ds(pl.multiple_of(chunk * CHUNK, CHUNK), CHUNK)
        before = held[...] + lax.dot_general(
            features_ref[:, lanes],
            feature_weight_ref[...],
            (((0,), (0,)), ((), ())),
            preferred_element_type=jnp.float32,
        )
        hidden = silu(before).astype(jnp.bfloat16)
        ids = lax.broadcasted_iota(jnp.int32, (nodes, CHUNK), 0)
        one_hot = jnp.where(ids == recv_row_ref[:, lanes], 1.0, 0.0).astype(jnp.bfloat16)
        widened = jnp.concatenate([hidden, jnp.ones((CHUNK, width), jnp.bfloat16)], axis=1)
        total[...] += jnp.dot(one_hot, widened, preferred_element_type=jnp.float32)

    gather(0, even)

    def pair(n, carry):
        gather(2 * n + 1, odd)
        add_up(2 * n, even)
        gather(jnp.minimum(2 * n + 2, chunks - 1), even)
        add_up(2 * n + 1, odd)
        return carry

    lax.fori_loop(0, chunks // 2, pair, 0)
    out_ref[...] = total[...]


def node_sums(send, recv, own, low, high, recv_terms, features, feature_weight):
    edges = send.shape[0]
    nodes, width = recv_terms.shape
    table_rows = own.shape[0] + 2 * low.shape[0]
    vmem = pl.BlockSpec(memory_space=pltpu.VMEM)
    smem = pl.BlockSpec(memory_space=pltpu.SMEM)
    hbm = pl.BlockSpec(memory_space=pl.ANY)
    return pl.pallas_call(
        edge_kernel,
        in_specs=[smem, smem, hbm, hbm, hbm, vmem, vmem, vmem, vmem],
        out_specs=vmem,
        out_shape=jax.ShapeDtypeStruct((nodes, 2 * width), jnp.float32),
        scratch_shapes=[
            pltpu.VMEM((table_rows, width), jnp.float32),
            pltpu.VMEM((CHUNK, width), jnp.float32),
            pltpu.VMEM((CHUNK, width), jnp.float32),
            pltpu.VMEM((nodes, 2 * width), jnp.float32),
            pltpu.SemaphoreType.DMA((3,)),
        ],
        compiler_params=pltpu.CompilerParams(vmem_limit_bytes=48 << 20),
        cost_estimate=pl.CostEstimate(
            flops=4 * edges * nodes * width,
            bytes_accessed=4 * table_rows * width,
            transcendentals=edges * width,
        ),
    )(send, recv, own, low, high, recv_terms, recv.reshape(1, -1), features, feature_weight)


def on_device(
    grid_inputs,
    embed_weight,
    embed_bias,
    mesh_latent,
    edge_features,
    senders,
    receivers,
    sender_weight,
    receiver_weight,
    feature_weight,
    hidden_bias,
    message_weight,
    message_bias,
    norm_gain,
    norm_shift,
):
    lon_count = lax.axis_size("lon")
    lon_place = lax.axis_index("lon")
    ch_count = lax.axis_size("ch")
    ch_place = lax.axis_index("ch")
    columns = grid_inputs.shape[0] // LAT
    mesh_nodes, share_width = mesh_latent.shape
    full_width = message_weight.shape[1]

    halo_terms = sender_terms(
        grid_inputs, embed_weight, embed_bias, sender_weight, LAT, 2 * HALO,
        lambda i: jnp.where(i < HALO, i, columns - 2 * HALO + i), jnp.bfloat16,
    )
    forward = [(i, (i + 1) % lon_count) for i in range(lon_count)]
    backward = [(target, source) for source, target in forward]
    low = lax.ppermute(halo_terms[HALO * LAT:], "lon", forward)
    high = lax.ppermute(halo_terms[:HALO * LAT], "lon", backward)
    packed = jnp.concatenate([mesh_latent, message_weight.reshape(-1, share_width)], axis=0)
    gathered = lax.all_gather(packed, "ch", axis=0)
    full_mesh = jnp.swapaxes(gathered[:, :mesh_nodes], 0, 1).reshape(mesh_nodes, full_width)
    full_message = gathered[:, mesh_nodes:].reshape(full_width, full_width)

    group = max(n for n in (1, 2, 3) if columns % n == 0)
    own = sender_terms(
        grid_inputs, embed_weight, embed_bias, sender_weight, group * LAT, columns // group,
        lambda i: i, jnp.float32,
    )
    recv_terms = (
        jnp.dot(full_mesh, receiver_weight, preferred_element_type=jnp.float32) + hidden_bias
    )
    grid_column = senders // LAT
    shifted = jnp.mod(grid_column - lon_place * columns + HALO, columns * lon_count)
    local_send = shifted * LAT + senders % LAT
    local_recv = receivers - lon_place * mesh_nodes
    pad = 16 - edge_features.shape[0]
    sums = node_sums(
        local_send, local_recv, own, low.astype(jnp.float32), high.astype(jnp.float32),
        recv_terms, jnp.pad(edge_features, ((0, pad), (0, 0))),
        jnp.pad(feature_weight, ((0, pad), (0, 0))),
    )
    part = mesh_nodes // ch_count
    mine = lax.all_to_all(
        sums[:, :share_width], "ch", split_axis=0, concat_axis=1, tiled=True
    )
    tallies = lax.dynamic_slice_in_dim(sums[:, share_width:share_width + 1], ch_place * part, part, 0)
    aggregated = (
        jnp.dot(mine, full_message.astype(jnp.float32), precision=lax.Precision.HIGHEST)
        + tallies * message_bias
    )
    centre = jnp.mean(aggregated, axis=1, keepdims=True)
    spread = jnp.mean(jnp.square(aggregated - centre), axis=1, keepdims=True)
    normed = (aggregated - centre) * lax.rsqrt(spread + 1.0)
    share = lax.all_to_all(normed, "ch", split_axis=1, concat_axis=0, tiled=True)
    return (mesh_latent.astype(jnp.float32) + share * norm_gain + norm_shift).astype(jnp.bfloat16)


def solution(mesh):
    return jax.shard_map(
        on_device,
        mesh=mesh,
        in_specs=(
            P("lon", None),
            P(),
            P(),
            P("lon", "ch"),
            P(None, "lon"),
            P("lon"),
            P("lon"),
            P(None, "ch"),
            P(None, "ch"),
            P(None, "ch"),
            P("ch"),
            P("ch", None),
            P(),
            P("ch"),
            P("ch"),
        ),
        out_specs=P("lon", "ch"),
        check_vma=False,
    )
```

time: 418 us -> 189 us (0.45)
  local copies, waits for them, and re-layouts: 191 us -> 46 us
  Pallas kernels: 0 us -> 96.3 us
  matrix products: 88.5 us -> 1.99 us
  waiting for transfers between devices: 72.6 us -> 5.06 us
  other arithmetic: 23.9 us -> 4.95 us
  blocking collectives: 19.6 us -> 9.08 us
    gather x22 -> x0, local copies, waits for them, and re-layouts: 185 us -> none  [the longest x11 125 us: accumulate(): jnp.take(sent_terms, send_ids, axis=0)]
    pallas_call x0 -> x3, Pallas kernels: none -> 96.3 us  [the longest x1 57 us: node_sums(): pl.pallas_call(edge_kernel, in_specs=[smem, smem, hbm, hbm, hbm, vmem, vm...]
    dot_general x14 -> x1, matrix products: 88.1 us -> 0.54 us  [on_device(): jnp.dot(mine, full_message.astype(jnp.float32), precision=lax.Precision.H...]
    ppermute x2, waiting for transfers between devices: 46.8 us -> 0.01 us  [the longest x1 0.01 us: on_device(): high = lax.ppermute(halo_terms[:HALO * LAT], 'lon', backward)]
    unnamed x24 -> x37, local copies, waits for them, and re-layouts: 1.08 us -> 39.2 us
    reduce_scatter x1 -> x0, waiting for transfers between devices: 25.8 us -> none  [on_device(): lax.psum_scatter(partial_value, 'ch', scatter_dimension=1, tiled=True)]
    psum x2 -> x0, blocking collectives: 11.4 us -> none  [the longest x1 5.76 us: on_device(): lax.psum(jnp.sum(node_share, axis=1, keepdims=True), 'ch') / full_width]
    concatenate x1, other arithmetic: 10.9 us -> 0.73 us  [on_device(): jnp.concatenate([mesh_latent, message_weight.reshape(-1, share_width)], a...]
  transfers between devices with their start and end apart: 3 -> 4, of which waited for: 3 -> 1; matrix products, arithmetic and copies ran while one was open for 0% -> 3% of each run, Pallas kernels for 0% -> 16%
where the time goes in v1:
time: 189 us; the launch traced here: 187 us
  Pallas kernels  96.3 us (51%)
  local copies, waits for them, and re-layouts  46 us (24%)
  between operations  13.7 us (7%)
  starting transfers between devices  9.61 us (5%)
  blocking collectives  9.08 us (5%)
  waiting for transfers between devices  5.06 us (3%)
  other arithmetic  4.95 us (3%)
  matrix products  1.99 us (1%)
    pallas_call x1, Pallas kernels, node_sums(): pl.pallas_call(edge_kernel, in_specs=[smem, smem, hbm, hbm, hbm, vmem, vm...  57 us
    pallas_call x2, Pallas kernels, sender_terms(): pl.pallas_call(dense_kernel, grid=(steps,), in_specs=[pl.BlockSpec((rows,...  39.3 us
    unnamed x37, local copies, waits for them, and re-layouts  39.2 us
    all_to_all x1, blocking collectives, on_device(): lax.all_to_all(normed, 'ch', split_axis=1, concat_axis=0, tiled=True)  9.08 us
    all_to_all x1, waiting for transfers between devices, on_device(): lax.all_to_all(sums[:, :share_width], 'ch', split_axis=0, concat_axis=1,...  5.02 us
    transpose x2, local copies, waits for them, and re-layouts, on_device(): jnp.swapaxes(gathered[:, :mesh_nodes], 0, 1).reshape(mesh_nodes, full_width)  4.17 us
  transfers between devices with their start and end apart: 4, of which 1 were waited for; matrix products, arithmetic and copies ran while one was open for 3% of the time, Pallas kernels for 16%

profile of v1, /device:TPU:0, one launch (start us, length us, event | category | flops | bytes accessed | tf_op | source)
XLA Modules:
  0.0 186.7 jit_solution(12489500219033700522)
XLA Ops:
  6.5 0.0 copy-start
  6.5 0.0 all-gather.3.cloned.1.call-start
  6.6 36.5 %copy.28.x_ref = bf16[28800,474]{1,0:T(8,128)(2,1)} copy(bf16[28800,474]{0,1:T(8,128)(2,1)} %param.15) | data formatting | bytes 54604800 | tf_op args[0]
  43.1 0.0 copy-done.2
  43.1 0.0 copy-done.6
  43.1 0.0 copy-done.3
  43.1 8.6 %shard_map.146 = bf16[5120,128]{1,0:T(8,128)(2,1)S(1)} custom-call(bf16[28800,474]{1,0:T(8,128)(2,1)} %copy.28.x_ref, bf16[474,512]{1,0:T(8,128)(2,1)S(1)} %copy-done.2, f32[1,512]{1,0:T(1,128)S(1)} %bitcast.36, bf16[512,128]{1,0:T(8,128)(2,1)S(1)} %copy-done.3), custom_call_target="tpu_custom_call" | custom-call | flops 3156213760 | bytes 7475200 | tf_op jit(solution)/shard_map/pallas_call | solution.py:34
  51.7 0.0 copy-start.10
  51.7 0.0 copy-start.7
  51.8 0.0 copy-start.9
  51.8 0.1 fusion.11
  51.9 0.0 copy-start.14
  51.9 3.0 %collective-permute-start = (bf16[2560,128]{1,0:T(8,128)(2,1)S(1)}, bf16[2560,128]{1,0:T(8,128)(2,1)}, u32[]{:S(2)}, u32[]{:S(2)}) collective-permute-start(bf16[2560,128]{1,0:T(8,128)(2,1)S(1)} %get-tuple-element.6), channel_id=1, source_target_pairs={{0,4},{4,8},{8,12},{12,16},{16,20},{20,24},{24,28},{28,0},{1,5},{5... | collective-permute-start | bytes 1966088 | tf_op jit(solution)/shard_map/ppermute | solution.py:181
  54.9 3.1 %collective-permute-start.1 = (bf16[2560,128]{1,0:T(8,128)(2,1)S(1)}, bf16[2560,128]{1,0:T(8,128)(2,1)}, u32[]{:S(2)}, u32[]{:S(2)}) collective-permute-start(bf16[2560,128]{1,0:T(8,128)(2,1)S(1)} %get-tuple-element.5), channel_id=1, source_target_pairs={{4,0},{8,4},{12,8},{16,12},{20,16},{24,20},{28,24},{0,28},{5,1},{9... | collective-permute-start | bytes 1966088 | tf_op jit(solution)/shard_map/ppermute | solution.py:182
  58.0 0.0 copy-done.10
  58.0 0.1 reshape.39
  58.1 0.0 copy-done.7
  58.1 0.7 pad_maximum_fusion
  58.8 0.0 all-gather.3.cloned.1.call-update
  58.9 0.0 copy-done.9
  58.9 0.1 pad.8.features_ref
  59.0 0.0 copy-done.14
  59.0 0.0 copy-start.11
  59.0 0.0 copy-start.12
  59.0 30.7 %shard_map.145.own_ref = f32[28800,128]{1,0:T(8,128)} custom-call(bf16[28800,474]{1,0:T(8,128)(2,1)} %copy.28.x_ref, bf16[474,512]{1,0:T(8,128)(2,1)S(1)} %copy-done.2, f32[1,512]{1,0:T(1,128)S(1)} %bitcast.37, bf16[512,128]{1,0:T(8,128)(2,1)S(1)} %copy-done.3), custom_call_target="tpu_custom_call" | custom-call | flops 17753702400 | bytes 42048000 | tf_op jit(solution)/shard_map/pallas_call | solution.py:34
  89.7 0.0 copy-done.11
  89.7 0.0 copy-done.12
  89.7 0.8 fusion.9
  90.5 0.0 collective-permute-done
  90.5 1.2 convert_element_type.18.low_ref
  91.7 0.0 collective-permute-done.1
  91.7 1.2 convert_element_type.19.high_ref
  92.9 0.0 all-gather.3.cloned.1.call-done
  92.9 0.0 copy-start.15
  92.9 2.0 %slice_bitcast_fusion = bf16[640,4,128]{2,0,1:T(8,128)(2,1)} fusion(bf16[4,1152,128]{2,1,0:T(8,128)(2,1)} %bitcast.39), kind=kLoop, calls=%fused_computation.2 | loop fusion | bytes 1310720 | tf_op jit(solution)/shard_map/transpose | solution.py:185
  94.9 2.2 %copy.30 = bf16[640,4,128]{0,2,1:T(8,128)(2,1)} copy(bf16[640,4,128]{2,0,1:T(8,128)(2,1)} %slice_bitcast_fusion) | data formatting | bytes 1310720 | tf_op jit(solution)/shard_map/transpose | solution.py:185
  97.1 0.0 copy-done
  97.1 0.0 copy-done.15
  97.1 1.5 convolution_add_fusion.recv_terms_ref
  98.6 0.0 copy-start.4
  98.6 0.9 copy-done.4
  99.5 0.9 copy-done.5
  100.3 57.0 %shard_map.147 = f32[640,256]{1,0:T(8,128)S(1)} custom-call(s32[22528]{0:T(1024)S(1)} %copy-done.4, s32[22528]{0:T(1024)S(1)} %copy-done.5, f32[28800,128]{1,0:T(8,128)} %shard_map.145.own_ref, f32[2560,128]{1,0:T(8,128)S(1)} %convert_element_type.18.low_ref, f32[2560,128]{1,0:T(8,128)S(1)} %convert_element_type.19.high_ref, ...), custom_call_target="tpu_custom_call" | custom-call | flops 7381975040 | bytes 17367040 | tf_op jit(solution)/shard_map/pallas_call | solution.py:129
  157.3 0.0 copy-start.1
  157.3 0.8 copy-done.1
  158.2 0.8 slice.27
  159.0 3.5 %all-to-all-start = ((f32[4,160,128]{2,1,0:T(8,128)}), f32[4,160,128]{2,1,0:T(8,128)S(1)}, u32[]{:S(2)}, u32[]{:S(2)}) async-start(f32[4,160,128]{2,1,0:T(8,128)} %bitcast.5), calls=%async_computation | async-start | bytes 655360 | tf_op jit(solution)/shard_map/all_to_all | solution.py:207
  162.4 0.0 slice-start
  162.4 0.0 copy-start.13
  162.4 1.1 slice.28
  163.6 0.3 reshape.42
  163.9 0.0 slice-done
  163.9 0.1 dynamic-slice_reduce_fusion
  164.0 0.0 copy-start.8
  164.0 0.0 copy-start.16
  164.1 0.0 copy-start.17
  164.1 5.0 %all-to-all-done = f32[4,160,128]{2,1,0:T(8,128)S(1)} async-done(((f32[4,160,128]{2,1,0:T(8,128)}), f32[4,160,128]{2,1,0:T(8,128)S(1)}, u32[]{:S(2)}, u32[]{:S(2)}) %all-to-all-start) | async-done | bytes 327712 | tf_op jit(solution)/shard_map/all_to_all | solution.py:207
  169.1 0.0 copy-done.13
  169.1 0.5 fusion.12
  169.6 0.2 multiply_reduce_fusion
  169.9 0.1 copy_bitcast_fusion
  170.0 9.1 %all_to_all.38 = f32[160,4,128]{2,0,1:T(8,128)S(1)} all-to-all(f32[160,4,128]{2,0,1:T(8,128)S(1)} %copy_bitcast_fusion), channel_id=1, replica_groups=mesh['lon'=8,'ch'=4] {'ch'}, dimensions={1} | all-to-all | bytes 655360 | tf_op jit(solution)/shard_map/all_to_all | solution.py:218
  179.1 0.0 copy-done.8
  179.1 0.7 fusion.4
  (9 shorter events, 0.0 us)
Async XLA Ops:
  6.5 90.6 %copy-start = (bf16[512,128]{1,0:T(8,128)(2,1)S(1)}, bf16[512,128]{1,0:T(8,128)(2,1)}, u32[]{:S(2)}) copy-start(bf16[512,128]{1,0:T(8,128)(2,1)} %param.23) | copy-start | bytes 393220
  6.5 36.6 %copy-start.2 = (bf16[474,512]{1,0:T(8,128)(2,1)S(1)}, bf16[474,512]{1,0:T(8,128)(2,1)}, u32[]{:S(2)}) copy-start(bf16[474,512]{1,0:T(8,128)(2,1)} %embed_ref.3) | copy-start | bytes 1456132
  6.5 36.6 %copy-start.6 = (f32[512]{0:T(512)S(1)}, f32[512]{0:T(512)}, u32[]{:S(2)}) copy-start(f32[512]{0:T(512)} %param.17) | copy-start | bytes 6148
  6.5 36.6 %copy-start.3 = (bf16[512,128]{1,0:T(8,128)(2,1)S(1)}, bf16[512,128]{1,0:T(8,128)(2,1)}, u32[]{:S(2)}) copy-start(bf16[512,128]{1,0:T(8,128)(2,1)} %sender_ref.3) | copy-start | bytes 393220
  6.5 86.4 %all-gather.3.cloned.1.call-start = ((), (), s32[]{:S(2)}) async-start(), calls=%async_computation.2 | async-start | bytes 1474560 | tf_op jit(solution)/shard_map/all_gather | solution.py:184
  51.7 6.3 %copy-start.10 = (bf16[128,512]{1,0:T(8,128)(2,1)S(1)}, bf16[128,512]{1,0:T(8,128)(2,1)}, u32[]{:S(2)}) copy-start(bf16[128,512]{1,0:T(8,128)(2,1)} %param.26) | copy-start | bytes 393220
  51.7 6.4 %copy-start.7 = (bf16[640,128]{1,0:T(8,128)(2,1)S(1)}, bf16[640,128]{1,0:T(8,128)(2,1)}, u32[]{:S(2)}) copy-start(bf16[640,128]{1,0:T(8,128)(2,1)} %param.18) | copy-start | bytes 491524
  51.8 7.1 %copy-start.9 = (bf16[4,22528]{1,0:T(4,128)(2,1)S(1)}, bf16[4,22528]{1,0:T(4,128)(2,1)}, u32[]{:S(2)}) copy-start(bf16[4,22528]{1,0:T(4,128)(2,1)} %param.19) | copy-start | bytes 540676
  51.9 7.1 %copy-start.14 = (bf16[4,128]{1,0:T(4,128)(2,1)S(1)}, bf16[4,128]{1,0:T(4,128)(2,1)}, u32[]{:S(2)}) copy-start(bf16[4,128]{1,0:T(4,128)(2,1)} %param.24) | copy-start | bytes 3076
  51.9 38.6 %collective-permute-start = (bf16[2560,128]{1,0:T(8,128)(2,1)S(1)}, bf16[2560,128]{1,0:T(8,128)(2,1)}, u32[]{:S(2)}, u32[]{:S(2)}) collective-permute-start(bf16[2560,128]{1,0:T(8,128)(2,1)S(1)} %get-tuple-element.6), channel_id=1, source_target_pairs={{0,4},{4,8},{8,12},{12,16},{16,20},{20,24},{24,28},{28,0},{1,5},{5... | collective-permute-start | bytes 1966088 | tf_op jit(solution)/shard_map/ppermute | solution.py:181
  54.9 36.8 %collective-permute-start.1 = (bf16[2560,128]{1,0:T(8,128)(2,1)S(1)}, bf16[2560,128]{1,0:T(8,128)(2,1)}, u32[]{:S(2)}, u32[]{:S(2)}) collective-permute-start(bf16[2560,128]{1,0:T(8,128)(2,1)S(1)} %get-tuple-element.5), channel_id=1, source_target_pairs={{4,0},{8,4},{12,8},{16,12},{20,16},{24,20},{28,24},{0,28},{5,1},{9... | collective-permute-start | bytes 1966088 | tf_op jit(solution)/shard_map/ppermute | solution.py:182
  59.0 30.7 %copy-start.11 = (s32[22528]{0:T(1024)S(1)}, s32[22528]{0:T(1024)}, u32[]{:S(2)}) copy-start(s32[22528]{0:T(1024)} %param.20) | copy-start | bytes 270340
  59.0 30.7 %copy-start.12 = (s32[22528]{0:T(1024)S(1)}, s32[22528]{0:T(1024)}, u32[]{:S(2)}) copy-start(s32[22528]{0:T(1024)} %param.21) | copy-start | bytes 270340
  92.9 4.2 %copy-start.15 = (f32[128]{0:T(128)S(1)}, f32[128]{0:T(128)}, u32[]{:S(2)}) copy-start(f32[128]{0:T(128)} %param.25) | copy-start | bytes 1540
  98.6 0.9 copy-start.4
  99.5 0.9 copy-start.5
  157.3 0.9 copy-start.1
  159.0 10.1 %all-to-all-start = ((f32[4,160,128]{2,1,0:T(8,128)}), f32[4,160,128]{2,1,0:T(8,128)S(1)}, u32[]{:S(2)}, u32[]{:S(2)}) async-start(f32[4,160,128]{2,1,0:T(8,128)} %bitcast.5), calls=%async_computation | async-start | bytes 655360 | tf_op jit(solution)/shard_map/all_to_all | solution.py:207
  162.4 1.5 slice-start
  162.4 6.7 %copy-start.13 = (f32[512]{0:T(512)S(1)}, f32[512]{0:T(512)}, u32[]{:S(2)}) copy-start(f32[512]{0:T(512)} %param.27) | copy-start | bytes 6148
  164.0 15.0 %copy-start.8 = (bf16[640,128]{1,0:T(8,128)(2,1)S(1)}, bf16[640,128]{1,0:T(8,128)(2,1)}, u32[]{:S(2)}) copy-start(bf16[640,128]{1,0:T(8,128)(2,1)} %param.18) | copy-start | bytes 491524
  164.0 15.0 %copy-start.16 = (f32[128]{0:T(128)S(1)}, f32[128]{0:T(128)}, u32[]{:S(2)}) copy-start(f32[128]{0:T(128)} %param.29) | copy-start | bytes 1540
  164.1 15.0 %copy-start.17 = (f32[128]{0:T(128)S(1)}, f32[128]{0:T(128)}, u32[]{:S(2)}) copy-start(f32[128]{0:T(128)} %param.28) | copy-start | bytes 1540
Sparse Core Ops, SparseCore 0:
  59.0 16.1 all-gather.2

commit v2 on v1

v2 whole, which is shorter than its diff:
```python
import functools

import jax
import jax.numpy as jnp
from jax import lax
from jax.experimental import pallas as pl
from jax.experimental.pallas import tpu as pltpu
from jax.sharding import PartitionSpec as P

LAT = 640
HALO = 4
CHUNK = 256


def silu(v):
    half = 0.5 * v
    return half + half * jnp.tanh(half)


def dense_kernel(
    steps,
    x_ref,
    embed_ref,
    bias_ref,
    sender_ref,
    mesh_ref,
    message_ref,
    out_ref,
    low_ref,
    high_ref,
    mesh_all_ref,
    message_all_ref,
    first_columns,
    last_columns,
    gather_send,
    gather_recv,
    halo_send,
    halo_recv,
    local_sem,
):
    step = pl.program_id(0)
    lon_count, ch_count = lax.axis_size("lon"), lax.axis_size("ch")
    lon_place, ch_place = lax.axis_index("lon"), lax.axis_index("ch")
    right = lax.rem(lon_place + 1, lon_count)
    left = lax.rem(lon_place + lon_count - 1, lon_count)
    halo_rows = low_ref.shape[0]
    pairs = ((mesh_ref, mesh_all_ref), (message_ref, message_all_ref))
    local = [
        pltpu.make_async_copy(ref, all_ref.at[ch_place], local_sem.at[n])
        for n, (ref, all_ref) in enumerate(pairs)
    ]
    partners = [lax.rem(ch_place + j, ch_count) for j in range(1, ch_count)]
    gathers = [
        pltpu.make_async_remote_copy(
            src_ref=ref,
            dst_ref=all_ref.at[ch_place],
            send_sem=gather_send.at[n, j],
            recv_sem=gather_recv.at[n, j],
            device_id={"ch": partner},
            device_id_type=pl.DeviceIdType.MESH,
        )
        for n, (ref, all_ref) in enumerate(pairs)
        for j, partner in enumerate(partners)
    ]
    halos = [
        pltpu.make_async_remote_copy(
            src_ref=src,
            dst_ref=dst,
            send_sem=halo_send.at[n],
            recv_sem=halo_recv.at[n],
            device_id={"lon": side},
            device_id_type=pl.DeviceIdType.MESH,
        )
        for n, (src, dst, side) in enumerate(
            ((last_columns, low_ref, right), (first_columns, high_ref, left))
        )
    ]

    @pl.when(step == 0)
    def _():
        barrier = pltpu.get_barrier_semaphore()
        for partner in partners:
            pl.semaphore_signal(
                barrier, inc=1, device_id={"ch": partner}, device_id_type=pl.DeviceIdType.MESH
            )
        for side in (left, right):
            pl.semaphore_signal(
                barrier, inc=1, device_id={"lon": side}, device_id_type=pl.DeviceIdType.MESH
            )
        pl.semaphore_wait(barrier, ch_count + 1)
        for copy in gathers + local:
            copy.start()

    @pl.when(step == 2)
    def _():
        for copy in halos:
            copy.start()

    before = (
        lax.dot_general(
            x_ref[...], embed_ref[...], (((0,), (0,)), ((), ())),
            preferred_element_type=jnp.float32,
        )
        + bias_ref[...]
    )
    latent = silu(before).astype(jnp.bfloat16)
    out_ref[...] = jnp.dot(latent, sender_ref[...], preferred_element_type=jnp.float32)

    @pl.when(step == 0)
    def _():
        first_columns[...] = out_ref[:halo_rows, :].astype(jnp.bfloat16)

    @pl.when(step == 1)
    def _():
        last_columns[...] = out_ref[out_ref.shape[0] - halo_rows:, :].astype(jnp.bfloat16)

    @pl.when(step == steps - 1)
    def _():
        for copy in gathers + halos + local:
            copy.wait()


def sender_terms(
    grid_inputs, embed_weight, embed_bias, sender_weight, mesh_latent, message_weight
):
    channels, full_width = embed_weight.shape
    width = sender_weight.shape[1]
    points = grid_inputs.shape[0]
    columns = points // LAT
    group = max(n for n in range(1, 6) if columns % n == 0)
    steps = columns // group
    assert group >= HALO and steps > 2
    rows = group * LAT
    ch_count = lax.axis_size("ch")

    def place(i):
        return jnp.where(i == 1, steps - 1, jnp.maximum(i - 1, 0))

    whole = lambda shape: pl.BlockSpec(shape, lambda i: (0, 0))
    hbm = pl.BlockSpec(memory_space=pl.ANY)
    halo = (HALO * LAT, width)
    return pl.pallas_call(
        functools.partial(dense_kernel, steps),
        grid=(steps,),
        in_specs=[
            pl.BlockSpec((channels, rows), lambda i: (0, place(i))),
            whole((channels, full_width)),
            whole((1, full_width)),
            whole((full_width, width)),
            hbm,
            hbm,
        ],
        out_specs=[pl.BlockSpec((rows, width), lambda i: (place(i), 0)), hbm, hbm, hbm, hbm],
        out_shape=[
            jax.ShapeDtypeStruct((points, width), jnp.float32),
            jax.ShapeDtypeStruct(halo, jnp.bfloat16),
            jax.ShapeDtypeStruct(halo, jnp.bfloat16),
            jax.ShapeDtypeStruct((ch_count, *mesh_latent.shape), jnp.bfloat16),
            jax.ShapeDtypeStruct((ch_count, *message_weight.shape), jnp.bfloat16),
        ],
        scratch_shapes=[
            pltpu.VMEM(halo, jnp.bfloat16),
            pltpu.VMEM(halo, jnp.bfloat16),
            pltpu.SemaphoreType.DMA((2, ch_count - 1)),
            pltpu.SemaphoreType.DMA((2, ch_count - 1)),
            pltpu.SemaphoreType.DMA((2,)),
            pltpu.SemaphoreType.DMA((2,)),
            pltpu.SemaphoreType.DMA((2,)),
        ],
        compiler_params=pltpu.CompilerParams(
            vmem_limit_bytes=56 << 20, collective_id=0, has_side_effects=True
        ),
        cost_estimate=pl.CostEstimate(
            flops=2 * points * full_width * (channels + width),
            bytes_accessed=points * (2 * channels + 4 * width),
            transcendentals=points * full_width,
        ),
    )(grid_inputs.T, embed_weight, embed_bias.reshape(1, -1), sender_weight,
      mesh_latent, message_weight)


def edge_kernel(
    send_ref,
    recv_ref,
    own_ref,
    low_ref,
    high_ref,
    mesh_all_ref,
    receiver_ref,
    hidden_bias_ref,
    recv_row_ref,
    features_ref,
    feature_weight_ref,
    out_ref,
    table,
    recv_terms_ref,
    even,
    odd,
    total,
    sem,
):
    own_rows = own_ref.shape[0]
    halo_rows = low_ref.shape[0]
    copy = pltpu.make_async_copy(own_ref, table.at[pl.ds(halo_rows, own_rows)], sem)
    copy.start()
    table[:halo_rows, :] = low_ref[...].astype(jnp.float32)
    table[halo_rows + own_rows:, :] = high_ref[...].astype(jnp.float32)
    parts, nodes, part_width = mesh_all_ref.shape
    recv_terms_ref[...] = hidden_bias_ref[...] + sum(
        jnp.dot(
            mesh_all_ref[n],
            receiver_ref[n * part_width:(n + 1) * part_width, :],
            preferred_element_type=jnp.float32,
        )
        for n in range(parts)
    )
    total[...] = jnp.zeros_like(total)
    copy.wait()
    chunks = recv_row_ref.shape[1] // CHUNK
    width = recv_terms_ref.shape[1]

    def gather(chunk, held):
        base = chunk * CHUNK
        for i in range(CHUNK):
            held[pl.ds(i, 1), :] = (
                table[pl.ds(send_ref[base + i], 1), :]
                + recv_terms_ref[pl.ds(recv_ref[base + i], 1), :]
            )

    def add_up(chunk, held):
        lanes = pl.ds(pl.multiple_of(chunk * CHUNK, CHUNK), CHUNK)
        before = held[...] + lax.dot_general(
            features_ref[:, lanes],
            feature_weight_ref[...],
            (((0,), (0,)), ((), ())),
            preferred_element_type=jnp.float32,
        )
        hidden = silu(before).astype(jnp.bfloat16)
        ids = lax.broadcasted_iota(jnp.int32, (nodes, CHUNK), 0)
        one_hot = jnp.where(ids == recv_row_ref[:, lanes], 1.0, 0.0).astype(jnp.bfloat16)
        widened = jnp.concatenate([hidden, jnp.ones((CHUNK, width), jnp.bfloat16)], axis=1)
        total[...] += jnp.dot(one_hot, widened, preferred_element_type=jnp.float32)

    gather(0, even)

    def pair(n, carry):
        gather(2 * n + 1, odd)
        add_up(2 * n, even)
        gather(jnp.minimum(2 * n + 2, chunks - 1), even)
        add_up(2 * n + 1, odd)
        return carry

    lax.fori_loop(0, chunks // 2, pair, 0)
    out_ref[...] = total[...]


def node_sums(
    send, recv, own, low, high, mesh_all, receiver_weight, hidden_bias, features, feature_weight
):
    edges = send.shape[0]
    parts, nodes, width = mesh_all.shape
    table_rows = own.shape[0] + 2 * low.shape[0]
    vmem = pl.BlockSpec(memory_space=pltpu.VMEM)
    smem = pl.BlockSpec(memory_space=pltpu.SMEM)
    hbm = pl.BlockSpec(memory_space=pl.ANY)
    return pl.pallas_call(
        edge_kernel,
        in_specs=[smem, smem, hbm] + [vmem] * 8,
        out_specs=vmem,
        out_shape=jax.ShapeDtypeStruct((nodes, 2 * width), jnp.float32),
        scratch_shapes=[
            pltpu.VMEM((table_rows, width), jnp.float32),
            pltpu.VMEM((nodes, width), jnp.float32),
            pltpu.VMEM((CHUNK, width), jnp.float32),
            pltpu.VMEM((CHUNK, width), jnp.float32),
            pltpu.VMEM((nodes, 2 * width), jnp.float32),
            pltpu.SemaphoreType.DMA,
        ],
        compiler_params=pltpu.CompilerParams(vmem_limit_bytes=48 << 20),
        cost_estimate=pl.CostEstimate(
            flops=4 * edges * nodes * width,
            bytes_accessed=4 * table_rows * width,
            transcendentals=edges * width,
        ),
    )(send, recv, own, low, high, mesh_all, receiver_weight, hidden_bias.reshape(1, -1),
      recv.reshape(1, -1), features, feature_weight)


def on_device(
    grid_inputs,
    embed_weight,
    embed_bias,
    mesh_latent,
    edge_features,
    senders,
    receivers,
    sender_weight,
    receiver_weight,
    feature_weight,
    hidden_bias,
    message_weight,
    message_bias,
    norm_gain,
    norm_shift,
):
    lon_count = lax.axis_size("lon")
    lon_place = lax.axis_index("lon")
    ch_count = lax.axis_size("ch")
    ch_place = lax.axis_index("ch")
    columns = grid_inputs.shape[0] // LAT
    mesh_nodes, share_width = mesh_latent.shape
    full_width = message_weight.shape[1]

    own, low, high, mesh_all, message_all = sender_terms(
        grid_inputs, embed_weight, embed_bias, sender_weight, mesh_latent, message_weight
    )
    full_message = message_all.reshape(full_width, full_width)
    grid_column = senders // LAT
    shifted = jnp.mod(grid_column - lon_place * columns + HALO, columns * lon_count)
    local_send = shifted * LAT + senders % LAT
    local_recv = receivers - lon_place * mesh_nodes
    pad = 16 - edge_features.shape[0]
    sums = node_sums(
        local_send, local_recv, own, low, high, mesh_all, receiver_weight, hidden_bias,
        jnp.pad(edge_features, ((0, pad), (0, 0))),
        jnp.pad(feature_weight, ((0, pad), (0, 0))),
    )
    part = mesh_nodes // ch_count
    mine = lax.all_to_all(
        sums[:, :share_width], "ch", split_axis=0, concat_axis=1, tiled=True
    )
    tallies = lax.dynamic_slice_in_dim(sums[:, share_width:share_width + 1], ch_place * part, part, 0)
    aggregated = (
        jnp.dot(mine, full_message.astype(jnp.float32), precision=lax.Precision.HIGHEST)
        + tallies * message_bias
    )
    centre = jnp.mean(aggregated, axis=1, keepdims=True)
    spread = jnp.mean(jnp.square(aggregated - centre), axis=1, keepdims=True)
    normed = (aggregated - centre) * lax.rsqrt(spread + 1.0)
    share = lax.all_to_all(normed, "ch", split_axis=1, concat_axis=0, tiled=True)
    return (mesh_latent.astype(jnp.float32) + share * norm_gain + norm_shift).astype(jnp.bfloat16)


def solution(mesh):
    return jax.shard_map(
        on_device,
        mesh=mesh,
        in_specs=(
            P("lon", None),
            P(),
            P(),
            P("lon", "ch"),
            P(None, "lon"),
            P("lon"),
            P("lon"),
            P(None, "ch"),
            P(None, "ch"),
            P(None, "ch"),
            P("ch"),
            P("ch", None),
            P(),
            P("ch"),
            P("ch"),
        ),
        out_specs=P("lon", "ch"),
        check_vma=False,
    )
```

time: 189 us -> 129 us (0.68)
  local copies, waits for them, and re-layouts: 46 us -> 5.9 us
  between operations: 13.7 us -> 0.14 us
  starting transfers between devices: 9.61 us -> 3.45 us
  Pallas kernels: 96.3 us -> 100 us
  other arithmetic: 4.95 us -> 2.18 us
    unnamed x37 -> x20, local copies, waits for them, and re-layouts: 39.2 us -> 3.32 us
    ppermute x2 -> x0, starting transfers between devices: 6.12 us -> none  [the longest x1 3.11 us: on_device(): high = lax.ppermute(halo_terms[:HALO * LAT], 'lon', backward)]
    transpose x2 -> x0, local copies, waits for them, and re-layouts: 4.17 us -> none  [on_device(): jnp.swapaxes(gathered[:, :mesh_nodes], 0, 1).reshape(mesh_nodes, full_width)]
    pallas_call x3 -> x2, Pallas kernels: 96.3 us -> 100 us  [the longest x1 57 us: node_sums(): pl.pallas_call(edge_kernel, in_specs=[smem, smem, hbm] + [vmem] * 8, out_...]
    convert_element_type x2 -> x0, other arithmetic: 2.35 us -> none  [the longest x1 1.17 us: on_device(): low.astype(jnp.float32)]
  transfers between devices with their start and end apart: 4 -> 1, of which waited for: 1 -> 1; matrix products, arithmetic and copies ran while one was open for 3% -> 0% of each run, Pallas kernels for 16% -> 0%
where the time goes in v2:
time: 129 us; the launch traced here: 128 us
  Pallas kernels  100 us (78%)
  blocking collectives  9.08 us (7%)
  waiting for transfers between devices  6.52 us (5%)
  local copies, waits for them, and re-layouts  5.9 us (5%)
  starting transfers between devices  3.45 us (3%)
  other arithmetic  2.18 us (2%)
    pallas_call x1, Pallas kernels, node_sums(): pl.pallas_call(edge_kernel, in_specs=[smem, smem, hbm] + [vmem] * 8, out_...  57 us
    pallas_call x1, Pallas kernels, sender_terms(): pl.pallas_call(functools.partial(dense_kernel, steps), grid=(steps,), in_...  43.5 us
    all_to_all x1, blocking collectives, on_device(): lax.all_to_all(normed, 'ch', split_axis=1, concat_axis=0, tiled=True)  9.08 us
    all_to_all x1, waiting for transfers between devices, on_device(): lax.all_to_all(sums[:, :share_width], 'ch', split_axis=0, concat_axis=1,...  6.52 us
    all_to_all x1, starting transfers between devices, on_device(): lax.all_to_all(sums[:, :share_width], 'ch', split_axis=0, concat_axis=1,...  3.45 us
    unnamed x20, local copies, waits for them, and re-layouts  3.32 us
  transfers between devices with their start and end apart: 1, of which 1 were waited for; matrix products, arithmetic and copies ran while one was open for 0% of the time, Pallas kernels for 0%

profile of v2, /device:TPU:0, one launch (start us, length us, event | category | flops | bytes accessed | tf_op | source)
XLA Modules:
  0.0 128.2 jit_solution(5847276544670111294)
XLA Ops:
  0.0 0.7 pad.9.feature_weight_ref
  0.7 1.0 pad.8.features_ref
  1.7 1.1 fusion.9
  2.8 0.0 copy-start
  2.8 0.0 copy-start.1
  2.8 0.0 copy-start.6
  2.8 43.5 %shard_map.145 = (f32[28800,128]{1,0:T(8,128)}, bf16[2560,128]{1,0:T(8,128)(2,1)}, bf16[2560,128]{1,0:T(8,128)(2,1)}, bf16[4,640,128]{2,1,0:T(8,128)(2,1)}, bf16[4,128,512]{2,1,0:T(8,128)(2,1)}) custom-call(bf16[474,28800]{1,0:T(8,128)(2,1)} %bitcast.32, bf16[474,512]{1,0:T(8,128)(2,1)} %embed_ref.1, f32[1,512]{1,0:T(1,128)} %bitcast.33, ...), custom_call_target="tpu_custom_call" | custom-call | flops 17753702400 | bytes 42048000 | tf_op jit(solution)/shard_map/pallas_call | solution.py:142
  46.3 0.0 copy-start.7
  46.3 0.0 copy-start.8
  46.3 0.0 copy-start.9
  46.3 0.0 copy-done
  46.3 0.0 copy-done.1
  46.4 0.0 copy-start.2
  46.4 1.1 copy-done.2
  47.5 0.0 copy-start.3
  47.5 1.1 copy-done.3
  48.5 0.0 copy-start.4
  48.5 1.1 copy-done.4
  49.6 0.0 copy-start.5
  49.6 57.0 %shard_map.146 = f32[640,256]{1,0:T(8,128)S(1)} custom-call(s32[22528]{0:T(1024)S(1)} %get-tuple-element.17.send_ref, s32[22528]{0:T(1024)S(1)} %get-tuple-element.18.recv_ref, f32[28800,128]{1,0:T(8,128)} %get-tuple-element.10.own_ref, bf16[2560,128]{1,0:T(8,128)(2,1)S(1)} %copy-done.2, bf16[2560,128]{1,0:T(8,128)(2,1)S(1)} %copy-done.3, ...), custom_call_target="tpu_custom_call" | custom-call | flops 7381975040 | bytes 17367040 | tf_op jit(solution)/shard_map/pallas_call | solution.py:266
  106.6 0.8 slice.8
  107.4 3.5 %all-to-all-start = ((f32[4,160,128]{2,1,0:T(8,128)}), f32[4,160,128]{2,1,0:T(8,128)S(1)}, u32[]{:S(2)}, u32[]{:S(2)}) async-start(f32[4,160,128]{2,1,0:T(8,128)} %bitcast.4), calls=%async_computation | async-start | bytes 655360 | tf_op jit(solution)/shard_map/all_to_all | solution.py:329
  110.9 0.1 dynamic-slice_reduce_fusion
  111.0 6.5 %all-to-all-done = f32[4,160,128]{2,1,0:T(8,128)S(1)} async-done(((f32[4,160,128]{2,1,0:T(8,128)}), f32[4,160,128]{2,1,0:T(8,128)S(1)}, u32[]{:S(2)}, u32[]{:S(2)}) %all-to-all-start) | async-done | bytes 327712 | tf_op jit(solution)/shard_map/all_to_all | solution.py:329
  117.5 0.0 copy-done.7
  117.5 0.0 copy-done.5
  117.5 0.5 fusion.11
  118.1 0.2 multiply_reduce_fusion
  118.3 0.1 copy_bitcast_fusion
  118.4 9.1 %all_to_all.35 = f32[160,4,128]{2,0,1:T(8,128)S(1)} all-to-all(f32[160,4,128]{2,0,1:T(8,128)S(1)} %copy_bitcast_fusion), channel_id=1, replica_groups=mesh['lon'=8,'ch'=4] {'ch'}, dimensions={1} | all-to-all | bytes 655360 | tf_op jit(solution)/shard_map/all_to_all | solution.py:340
  127.5 0.0 copy-done.6
  127.5 0.0 copy-done.8
  127.5 0.0 copy-done.9
  127.5 0.7 fusion.3
  (3 shorter events, 0.0 us)
Async XLA Ops:
  2.8 43.5 %copy-start = (bf16[512,128]{1,0:T(8,128)(2,1)S(1)}, bf16[512,128]{1,0:T(8,128)(2,1)}, u32[]{:S(2)}) copy-start(bf16[512,128]{1,0:T(8,128)(2,1)} %receiver_ref.1) | copy-start | bytes 393220
  2.8 43.5 %copy-start.1 = (f32[128]{0:T(128)S(1)}, f32[128]{0:T(128)}, u32[]{:S(2)}) copy-start(f32[128]{0:T(128)} %param.25) | copy-start | bytes 1540
  2.8 124.7 %copy-start.6 = (bf16[640,128]{1,0:T(8,128)(2,1)S(1)}, bf16[640,128]{1,0:T(8,128)(2,1)}, u32[]{:S(2)}) copy-start(bf16[640,128]{1,0:T(8,128)(2,1)} %mesh_ref.1) | copy-start | bytes 491524
  46.3 71.2 %copy-start.7 = (f32[512]{0:T(512)S(1)}, f32[512]{0:T(512)}, u32[]{:S(2)}) copy-start(f32[512]{0:T(512)} %param.27) | copy-start | bytes 6148
  46.3 81.2 %copy-start.8 = (f32[128]{0:T(128)S(1)}, f32[128]{0:T(128)}, u32[]{:S(2)}) copy-start(f32[128]{0:T(128)} %param.29) | copy-start | bytes 1540
  46.3 81.2 %copy-start.9 = (f32[128]{0:T(128)S(1)}, f32[128]{0:T(128)}, u32[]{:S(2)}) copy-start(f32[128]{0:T(128)} %param.28) | copy-start | bytes 1540
  46.4 1.1 copy-start.2
  47.5 1.1 copy-start.3
  48.5 1.1 copy-start.4
  49.6 67.9 %copy-start.5 = (bf16[4,128,512]{2,1,0:T(8,128)(2,1)S(1)}, bf16[4,128,512]{2,1,0:T(8,128)(2,1)}, u32[]{:S(2)}) copy-start(bf16[4,128,512]{2,1,0:T(8,128)(2,1)} %get-tuple-element.14) | copy-start | bytes 1572868
  107.4 10.1 %all-to-all-start = ((f32[4,160,128]{2,1,0:T(8,128)}), f32[4,160,128]{2,1,0:T(8,128)S(1)}, u32[]{:S(2)}, u32[]{:S(2)}) async-start(f32[4,160,128]{2,1,0:T(8,128)} %bitcast.4), calls=%async_computation | async-start | bytes 655360 | tf_op jit(solution)/shard_map/all_to_all | solution.py:329

commit v3 on v2

--- a/solution.py
+++ b/solution.py
@@ -72,7 +72,7 @@
             device_id_type=pl.DeviceIdType.MESH,
         )
         for n, (src, dst, side) in enumerate(
-            ((last_columns, low_ref, right), (first_columns, high_ref, left))
+            ((first_columns, high_ref, left), (last_columns, low_ref, right))
         )
     ]
 
@@ -91,10 +91,8 @@
         for copy in gathers + local:
             copy.start()
 
-    @pl.when(step == 2)
-    def _():
-        for copy in halos:
-            copy.start()
+    for n, copy in enumerate(halos):
+        pl.when(step == n + 1)(copy.start)
 
     before = (
         lax.dot_general(
@@ -192,6 +190,7 @@
     features_ref,
     feature_weight_ref,
     out_ref,
+    tally_ref,
     table,
     recv_terms_ref,
     even,
@@ -251,7 +250,8 @@
         return carry
 
     lax.fori_loop(0, chunks // 2, pair, 0)
-    out_ref[...] = total[...]
+    out_ref[...] = total[:, :width]
+    tally_ref[...] = total[:, width:]
 
 
 def node_sums(
@@ -266,8 +266,8 @@
     return pl.pallas_call(
         edge_kernel,
         in_specs=[smem, smem, hbm] + [vmem] * 8,
-        out_specs=vmem,
-        out_shape=jax.ShapeDtypeStruct((nodes, 2 * width), jnp.float32),
+        out_specs=[vmem, vmem],
+        out_shape=[jax.ShapeDtypeStruct((nodes, width), jnp.float32)] * 2,
         scratch_shapes=[
             pltpu.VMEM((table_rows, width), jnp.float32),
             pltpu.VMEM((nodes, width), jnp.float32),
@@ -286,6 +286,101 @@
       recv.reshape(1, -1), features, feature_weight)
 
 
+def tail_kernel(
+    totals_ref,
+    tally_ref,
+    message_ref,
+    message_bias_ref,
+    latent_ref,
+    gain_ref,
+    shift_ref,
+    out_ref,
+    got,
+    give,
+    back,
+    there_send,
+    there_recv,
+    back_send,
+    back_recv,
+):
+    ch_count = lax.axis_size("ch")
+    me = lax.axis_index("ch")
+    parts, part, width = got.shape
+    partners = [lax.rem(me + j, ch_count) for j in range(1, ch_count)]
+    barrier = pltpu.get_barrier_semaphore()
+    for partner in partners:
+        pl.semaphore_signal(
+            barrier, inc=1, device_id={"ch": partner}, device_id_type=pl.DeviceIdType.MESH
+        )
+    pl.semaphore_wait(barrier, ch_count - 1)
+
+    def copy_to(source, target, sends, recvs, j, partner):
+        return pltpu.make_async_remote_copy(
+            src_ref=source,
+            dst_ref=target.at[me],
+            send_sem=sends.at[j],
+            recv_sem=recvs.at[j],
+            device_id={"ch": partner},
+            device_id_type=pl.DeviceIdType.MESH,
+        )
+
+    there = [
+        copy_to(totals_ref.at[partner], got, there_send, there_recv, j, partner)
+        for j, partner in enumerate(partners)
+    ]
+    for copy in there:
+        copy.start()
+    got[me] = totals_ref[me]
+    bias = tally_ref[me][:, :1] * message_bias_ref[...]
+    for copy in there:
+        copy.wait()
+    aggregated = bias
+    for n in range(parts):
+        rest = got[n]
+        for _ in range(3):
+            piece = rest.astype(jnp.bfloat16)
+            aggregated += jnp.dot(piece, message_ref[n], preferred_element_type=jnp.float32)
+            rest = rest - piece.astype(jnp.float32)
+    centre = jnp.mean(aggregated, axis=1, keepdims=True)
+    spread = jnp.mean(jnp.square(aggregated - centre), axis=1, keepdims=True)
+    normed = (aggregated - centre) * lax.rsqrt(spread + 1.0)
+    for n in range(parts):
+        give[n] = normed[:, n * width:(n + 1) * width]
+    back[me] = give[me]
+    returns = [
+        copy_to(give.at[partner], back, back_send, back_recv, j, partner)
+        for j, partner in enumerate(partners)
+    ]
+    for copy in returns:
+        copy.start()
+    for copy in returns:
+        copy.wait()
+    for n in range(parts):
+        rows = slice(n * part, (n + 1) * part)
+        out_ref[rows, :] = (
+            latent_ref[rows, :].astype(jnp.float32) + back[n] * gain_ref[...] + shift_ref[...]
+        ).astype(out_ref.dtype)
+
+
+def finished(totals, tallies, message_all, message_bias, mesh_latent, norm_gain, norm_shift):
+    nodes, width = mesh_latent.shape
+    ch_count = lax.axis_size("ch")
+    blocks = (ch_count, nodes // ch_count, width)
+    vmem = pl.BlockSpec(memory_space=pltpu.VMEM)
+    return pl.pallas_call(
+        tail_kernel,
+        in_specs=[vmem] * 7,
+        out_specs=vmem,
+        out_shape=jax.ShapeDtypeStruct((nodes, width), jnp.bfloat16),
+        scratch_shapes=[pltpu.VMEM(blocks, jnp.float32)] * 3
+        + [pltpu.SemaphoreType.DMA((ch_count - 1,))] * 4,
+        compiler_params=pltpu.CompilerParams(
+            vmem_limit_bytes=32 << 20, collective_id=1, has_side_effects=True
+        ),
+    )(totals.reshape(blocks), tallies.reshape(blocks), message_all, message_bias.reshape(1, -1),
+      mesh_latent, norm_gain.reshape(1, -1), norm_shift.reshape(1, -1))
+
+
 def on_device(
     grid_inputs,
     embed_weight,
@@ -305,40 +400,25 @@
 ):
     lon_count = lax.axis_size("lon")
     lon_place = lax.axis_index("lon")
-    ch_count = lax.axis_size("ch")
-    ch_place = lax.axis_index("ch")
     columns = grid_inputs.shape[0] // LAT
-    mesh_nodes, share_width = mesh_latent.shape
-    full_width = message_weight.shape[1]
+    mesh_nodes = mesh_latent.shape[0]
 
     own, low, high, mesh_all, message_all = sender_terms(
         grid_inputs, embed_weight, embed_bias, sender_weight, mesh_latent, message_weight
     )
-    full_message = message_all.reshape(full_width, full_width)
     grid_column = senders // LAT
     shifted = jnp.mod(grid_column - lon_place * columns + HALO, columns * lon_count)
     local_send = shifted * LAT + senders % LAT
     local_recv = receivers - lon_place * mesh_nodes
     pad = 16 - edge_features.shape[0]
-    sums = node_sums(
+    totals, tallies = node_sums(
         local_send, local_recv, own, low, high, mesh_all, receiver_weight, hidden_bias,
         jnp.pad(edge_features, ((0, pad), (0, 0))),
         jnp.pad(feature_weight, ((0, pad), (0, 0))),
     )
-    part = mesh_nodes // ch_count
-    mine = lax.all_to_all(
-        sums[:, :share_width], "ch", split_axis=0, concat_axis=1, tiled=True
-    )
-    tallies = lax.dynamic_slice_in_dim(sums[:, share_width:share_width + 1], ch_place * part, part, 0)
-    aggregated = (
-        jnp.dot(mine, full_message.astype(jnp.float32), precision=lax.Precision.HIGHEST)
-        + tallies * message_bias
-    )
-    centre = jnp.mean(aggregated, axis=1, keepdims=True)
-    spread = jnp.mean(jnp.square(aggregated - centre), axis=1, keepdims=True)
-    normed = (aggregated - centre) * lax.rsqrt(spread + 1.0)
-    share = lax.all_to_all(normed, "ch", split_axis=1, concat_axis=0, tiled=True)
-    return (mesh_latent.astype(jnp.float32) + share * norm_gain + norm_shift).astype(jnp.bfloat16)
+    return finished(
+        totals, tallies, message_all, message_bias, mesh_latent, norm_gain, norm_shift
+    )
 
 
 def solution(mesh):

time: 129 us -> 117 us (0.907)
  blocking collectives: 9.08 us -> 0 us
  Pallas kernels: 100 us -> 108 us
  waiting for transfers between devices: 6.52 us -> 0 us
  starting transfers between devices: 3.45 us -> 0 us
    pallas_call x0 -> x1, Pallas kernels: none -> 11 us  [finished(): pl.pallas_call(tail_kernel, in_specs=[vmem] * 7, out_specs=vmem, out_shap...]
    all_to_all x1 -> x0, blocking collectives: 9.08 us -> none  [on_device(): lax.all_to_all(normed, 'ch', split_axis=1, concat_axis=0, tiled=True)]
    all_to_all x1 -> x0, waiting for transfers between devices: 6.52 us -> none  [on_device(): lax.all_to_all(sums[:, :share_width], 'ch', split_axis=0, concat_axis=1,...]
    all_to_all x1 -> x0, starting transfers between devices: 3.45 us -> none  [on_device(): lax.all_to_all(sums[:, :share_width], 'ch', split_axis=0, concat_axis=1,...]
    pallas_call x1, Pallas kernels: 43.5 us -> 40.3 us  [sender_terms(): pl.pallas_call(functools.partial(dense_kernel, steps), grid=(steps,), in_...]
    unnamed x20 -> x21, local copies, waits for them, and re-layouts: 3.32 us -> 4.02 us
  transfers between devices with their start and end apart: 1 -> 0, of which waited for: 1 -> 0; matrix products, arithmetic and copies ran while one was open for 0% -> 0% of each run, Pallas kernels for 0% -> 0%
where the time goes in v3:
time: 117 us; the launch traced here: 115 us
  Pallas kernels  108 us (92%)
  local copies, waits for them, and re-layouts  5.7 us (5%)
    pallas_call x1, Pallas kernels, node_sums(): pl.pallas_call(edge_kernel, in_specs=[smem, smem, hbm] + [vmem] * 8, out_...  57 us
    pallas_call x1, Pallas kernels, sender_terms(): pl.pallas_call(functools.partial(dense_kernel, steps), grid=(steps,), in_...  40.3 us
    pallas_call x1, Pallas kernels, finished(): pl.pallas_call(tail_kernel, in_specs=[vmem] * 7, out_specs=vmem, out_shap...  11 us
    unnamed x21, local copies, waits for them, and re-layouts  4.02 us

profile of v3, /device:TPU:0, one launch (start us, length us, event | category | flops | bytes accessed | tf_op | source)
XLA Modules:
  0.0 115.3 jit_solution(16032474490628082832)
XLA Ops:
  0.0 0.7 pad.9.feature_weight_ref
  0.7 1.1 fusion.4
  1.8 1.0 pad.8.features_ref
  2.8 0.0 copy-start.5
  2.8 0.0 copy-start.6
  2.8 0.0 copy-start.1
  2.8 0.0 copy-start.2
  2.8 0.0 copy-start.3
  2.8 0.0 copy-start.4
  2.9 40.3 %shard_map.145 = (f32[28800,128]{1,0:T(8,128)}, bf16[2560,128]{1,0:T(8,128)(2,1)}, bf16[2560,128]{1,0:T(8,128)(2,1)}, bf16[4,640,128]{2,1,0:T(8,128)(2,1)}, bf16[4,128,512]{2,1,0:T(8,128)(2,1)}) custom-call(bf16[474,28800]{1,0:T(8,128)(2,1)} %bitcast.16, bf16[474,512]{1,0:T(8,128)(2,1)} %embed_ref.1, f32[1,512]{1,0:T(1,128)} %bitcast.17, ...), custom_call_target="tpu_custom_call" | custom-call | flops 17753702400 | bytes 42048000 | tf_op jit(solution)/shard_map/pallas_call | solution.py:140
  43.2 0.0 copy-start
  43.2 0.0 copy-done.5
  43.2 0.0 copy-done.6
  43.2 0.0 copy-start.7
  43.2 1.1 copy-done.7
  44.3 0.0 copy-start.8
  44.4 1.1 copy-done.8
  45.4 0.0 copy-start.9
  45.4 1.1 copy-done.9
  46.5 57.0 %shard_map.146 = (f32[640,128]{1,0:T(8,128)S(1)}, f32[640,128]{1,0:T(8,128)S(1)}) custom-call(s32[22528]{0:T(1024)S(1)} %get-tuple-element.19.send_ref, s32[22528]{0:T(1024)S(1)} %get-tuple-element.20.recv_ref, f32[28800,128]{1,0:T(8,128)} %get-tuple-element.12.own_ref, bf16[2560,128]{1,0:T(8,128)(2,1)S(1)} %copy-done.7, bf16[2560,128]{1,0:T(8,128)(2,1)S(1)} %copy-done.8, ...), custom_call_target="tpu_custom_call" | custom-call | flops 7381975040 | bytes 17367040 | tf_op jit(solution)/shard_map/pallas_call | solution.py:266
  103.5 0.0 copy-done.1
  103.6 0.0 copy-done.2
  103.6 0.0 copy-done.3
  103.6 0.0 copy-done.4
  103.6 0.0 copy-done
  103.6 11.0 %shard_map.147 = bf16[640,128]{1,0:T(8,128)(2,1)S(1)} custom-call(f32[4,160,128]{2,1,0:T(8,128)S(1)} %bitcast.9, f32[4,160,128]{2,1,0:T(8,128)S(1)} %bitcast.10, bf16[4,128,512]{2,1,0:T(8,128)(2,1)S(1)} %copy-done, f32[1,512]{1,0:T(1,128)S(1)} %bitcast.12, bf16[640,128]{1,0:T(8,128)(2,1)S(1)} %copy-done.1, f32[1,128]{1,0:T(1,128)S(1)} %bitcast.13, ...), custom_call_target="tpu_custom_call" | custom-call | tf_op jit(solution)/shard_map/pallas_call | solution.py:370
  114.6 0.7 copy.17
Async XLA Ops:
  2.8 40.4 %copy-start.5 = (bf16[512,128]{1,0:T(8,128)(2,1)S(1)}, bf16[512,128]{1,0:T(8,128)(2,1)}, u32[]{:S(2)}) copy-start(bf16[512,128]{1,0:T(8,128)(2,1)} %receiver_ref.1) | copy-start | bytes 393220
  2.8 40.4 %copy-start.6 = (f32[128]{0:T(128)S(1)}, f32[128]{0:T(128)}, u32[]{:S(2)}) copy-start(f32[128]{0:T(128)} %param.25) | copy-start | bytes 1540
  2.8 100.7 %copy-start.1 = (bf16[640,128]{1,0:T(8,128)(2,1)S(1)}, bf16[640,128]{1,0:T(8,128)(2,1)}, u32[]{:S(2)}) copy-start(bf16[640,128]{1,0:T(8,128)(2,1)} %latent_ref.1) | copy-start | bytes 491524
  2.8 100.7 %copy-start.2 = (f32[512]{0:T(512)S(1)}, f32[512]{0:T(512)}, u32[]{:S(2)}) copy-start(f32[512]{0:T(512)} %param.27) | copy-start | bytes 6148
  2.8 100.7 %copy-start.3 = (f32[128]{0:T(128)S(1)}, f32[128]{0:T(128)}, u32[]{:S(2)}) copy-start(f32[128]{0:T(128)} %param.28) | copy-start | bytes 1540
  2.8 100.7 %copy-start.4 = (f32[128]{0:T(128)S(1)}, f32[128]{0:T(128)}, u32[]{:S(2)}) copy-start(f32[128]{0:T(128)} %param.29) | copy-start | bytes 1540
  43.2 60.4 %copy-start = (bf16[4,128,512]{2,1,0:T(8,128)(2,1)S(1)}, bf16[4,128,512]{2,1,0:T(8,128)(2,1)}, u32[]{:S(2)}) copy-start(bf16[4,128,512]{2,1,0:T(8,128)(2,1)} %get-tuple-element.18.message_ref) | copy-start | bytes 1572868
  43.2 1.1 copy-start.7
  44.3 1.1 copy-start.8
  45.4 1.1 copy-start.9
